TPU v7x, 32 devices: a whole 2x2x4 slice. The times are simulated.
32 devices in a mesh: groups: 2 (over y), bank: 4 (over z), freq: 2 (over x), seg: 2 (over core).
Axes of the slice: x: 2, y: 2, z: 4, core: 2. Of those that a mesh axis runs over, the one named last changes fastest.
Arguments:
- coarse_spectra: bfloat16 [64, 2, 16384], P(('groups', 'seg', 'bank'), None, 'freq'), parts along dimension 0, may hold values from -6 to 6
- fine_spectra: bfloat16 [64, 2, 65536], P(('groups', 'seg', 'bank'), None, 'freq'), parts along dimension 0, may hold values from -6 to 6
- coarse_templates: bfloat16 [2, 2048, 16384], P(None, 'bank', 'freq'), may hold values from -6 to 6
- fine_templates: bfloat16 [2, 4, 64, 65536], P(None, 'bank', None, 'freq'), may hold values from -6 to 6
- coarse_weight: float32 [32768], P(('groups', 'freq')), parts along dimension 0, may hold values from 0.2 to 2
- fine_weight: float32 [131072], P(('groups', 'freq')), parts along dimension 0, may hold values from 0.2 to 2
- triggers: int32 [64, 2], P(('groups', 'seg')), parts along dimension 0, may hold values from 0 to 3, all different within a row; in each aligned block of 4 rows (0 to 3, 4 to 7, ...) at most 2 rows name the same one
- offsets: int32 [64, 2], P(('groups', 'seg')), parts along dimension 0, may hold values from 0 to 131056
Outputs:
- coarse_snr: float32 [2048, 64], P(('bank', 'freq'), ('groups', 'seg')), parts along dimension 1
- fine_snr: float32 [64, 2, 64], P(('groups', 'seg', 'bank'), None, 'freq'), parts along dimension 0
There are 2 independent parts, one for each index of `groups`. A program takes and returns all parts, laid end to end along the dimension named above; an argument that names none is the same for every part. Nothing has to cross between parts.
Inputs may be any that keep to these rules, and one draw needn't show every extreme that they name: `triggers`: each segment names 2 different sub-banks. In each aligned block of 4 segments (the segments of one device along seg and bank) no sub-bank is named more than 2 times.
All inputs are finite; a program needn't handle non-finite values.
Results may differ from a plain program's by a relative error of at most 0.0021.
Values may be sent and summed in bfloat16 or wider, within the bound.
A program may use at most 128 MiB of HBM per device.

v0:
```python
import functools
import math

import jax
import jax.numpy as jnp
import numpy as np
from jax import lax
from jax.experimental import pallas as pl
from jax.experimental.pallas import tpu as pltpu
from jax.sharding import PartitionSpec as P

FC = 16384
FB = 65536
CAP = 2
LC = 16
LF = 16
CSTRIDE = 2047

MESH = pl.DeviceIdType.MESH
F32 = jnp.float32
BF16 = jnp.bfloat16


def phase_of(counts, period):
    radians = 2.0 * math.pi / period * counts.astype(jnp.float32)
    return (jnp.cos(radians), jnp.sin(radians))


def offset_count(freq_ids, offset, period):
    upper_bits = offset // 512
    lower_bits = offset % 512
    lower_term = freq_ids * lower_bits % period
    upper_term = freq_ids * upper_bits % (period // 512) * 512
    return (lower_term + upper_term) % period


def unit_table(count, stride, period):
    angle = 2.0 * np.pi * ((np.arange(count) * stride) % period) / period
    return np.stack([np.cos(angle), np.sin(angle)]).astype(np.float32)


def pair_slots(naming, capacity):
    ranking = jnp.cumsum(naming.astype(jnp.int32), axis=1) - 1
    columns = jnp.arange(capacity, dtype=jnp.int32)
    return naming[:, None, :] & (ranking[:, None, :] == columns[None, :, None])


def nt_dot(left, right):
    return lax.dot_general(left, right, (((1,), (1,)), ((), ())), preferred_element_type=F32)


def lag_rows(real, imag, step_re, step_im, lags):
    reals, imags, pend_re, pend_im = [], [], [], []
    for j in range(lags):
        pend_re.append(real)
        pend_im.append(imag)
        if j % 2 == 1:
            reals.append(jnp.concatenate(pend_re, axis=0).astype(BF16))
            imags.append(jnp.concatenate(pend_im, axis=0).astype(BF16))
            pend_re, pend_im = [], []
        if j + 1 < lags:
            real, imag = real * step_re - imag * step_im, real * step_im + imag * step_re
    return jnp.concatenate(reals, axis=0), jnp.concatenate(imags, axis=0)


def peak(energy, groups, width):
    total = energy.shape[1]
    while total > width:
        half = total // 2
        if half % 128 == 0:
            energy = jnp.maximum(energy[:, :half], energy[:, half:])
        else:
            energy = jnp.maximum(energy, pltpu.roll(energy, energy.shape[1] - half, 1))
        total = half
    return energy


def norm_add(acc, index, rows_of, weight, rows, width):
    group = 32
    for r in range(0, rows, group):
        part = None
        for c in range(0, width, 128):
            hr, hi = rows_of(r, group, c)
            hr = hr.astype(F32)
            hi = hi.astype(F32)
            term = (hr * hr + hi * hi) * weight[:, c : c + 128]
            part = term if part is None else part + term
        acc[index(r), pl.ds(r % acc.shape[1], group), :] += part


def kernel(
    cfg,
    coarse,
    fine,
    chooser,
    giver,
    ctemp,
    ftemp,
    cweight,
    fweight,
    ctable,
    ftable,
    shift_ac,
    shift_as,
    shift_bc,
    shift_bs,
    csnr,
    fout,
    cspec,
    outgoing,
    cstep,
    fstep,
    fsnr,
    back,
    ag,
    slots,
    cacc,
    cnorm,
    facc,
    fsum,
    fnorm,
    crecv,
    cnrecv,
    frecv,
    fnrecv,
    ag_send,
    ag_recv,
    sl_send,
    sl_recv,
    own_sem,
    cx_send,
    cx_recv,
    fx_send,
    fx_recv,
    bk_send,
    bk_recv,
):
    nb, nf, kc, kf, csteps, fsteps, sub, fsub = cfg
    step = pl.program_id(0)
    me = lax.axis_index("bank")
    fme = lax.axis_index("freq")
    segs = nb * (cspec.shape[0] // 2)
    seg_dev = cspec.shape[0] // 2
    slot_total = nb * CAP
    crow = cacc.shape[2]
    q = fsum.shape[2]
    nc = segs * LC
    nfl = slot_total * LF

    def ag_copy(d, chunk):
        window = pl.ds(pl.multiple_of(chunk * kc, kc), kc)
        return pltpu.make_async_remote_copy(
            src_ref=cspec.at[:, window],
            dst_ref=ag.at[me, :, window],
            send_sem=ag_send.at[d - 1, chunk],
            recv_sem=ag_recv.at[d - 1, chunk],
            device_id={"bank": lax.rem(me + d, nb)},
            device_id_type=MESH,
        )

    def slot_copy(d, chunk):
        peer = lax.rem(me + d, nb)
        window = pl.ds(pl.multiple_of(chunk * kf, kf), kf)
        return pltpu.make_async_remote_copy(
            src_ref=outgoing.at[peer, :, window],
            dst_ref=slots.at[me, :, window],
            send_sem=sl_send.at[d - 1, chunk],
            recv_sem=sl_recv.at[d - 1, chunk],
            device_id={"bank": peer},
            device_id_type=MESH,
        )

    def table_copies():
        cbins = coarse.shape[2]
        fbins = fine.shape[2]
        return (
            pltpu.make_async_copy(
                ctable.at[:, pl.ds(pl.multiple_of(fme * cbins, cbins), cbins)], cstep, own_sem.at[0]
            ),
            pltpu.make_async_copy(
                ftable.at[:, pl.ds(pl.multiple_of(fme * fbins, fbins), fbins)], fstep, own_sem.at[1]
            ),
        )

    def back_copies():
        return [
            pltpu.make_async_remote_copy(
                src_ref=fsnr,
                dst_ref=back.at[me],
                send_sem=bk_send.at[d - 1],
                recv_sem=bk_recv.at[d - 1],
                device_id={"bank": lax.rem(me + d, nb)},
                device_id_type=MESH,
            )
            for d in range(1, nb)
        ]

    def by_part(block):
        block = block.astype(F32)
        return jnp.concatenate([block[:, 0, :], block[:, 1, :]], axis=0)

    def freq_copies(pairs, send, recv):
        copies = []
        for d in range(1, nf):
            peer = lax.rem(fme + d, nf)
            for k, (source, target) in enumerate(pairs):
                copies.append(
                    pltpu.make_async_remote_copy(
                        src_ref=source.at[peer],
                        dst_ref=target.at[d - 1],
                        send_sem=send.at[d - 1, k],
                        recv_sem=recv.at[d - 1, k],
                        device_id={"freq": peer},
                        device_id_type=MESH,
                    )
                )
        return copies

    coarse_pairs = ((cacc, crecv), (cnorm, cnrecv))
    fine_pairs = ((fsum, frecv), (fnorm, fnrecv))

    @pl.when(step == 0)
    def _():
        barrier = pltpu.get_barrier_semaphore()
        for d in range(1, nb):
            pl.semaphore_signal(
                barrier, inc=1, device_id={"bank": lax.rem(me + d, nb)}, device_id_type=MESH
            )
        for d in range(1, nf):
            pl.semaphore_signal(
                barrier, inc=1, device_id={"freq": lax.rem(fme + d, nf)}, device_id_type=MESH
            )
        for copy in table_copies():
            copy.start()
        for c in range(0, coarse.shape[2], kc):
            cspec[:, c : c + kc] = by_part(coarse[:, :, c : c + kc]).astype(BF16)
        ag[me] = cspec[...]
        pl.semaphore_wait(barrier, nb - 1 + nf - 1)
        for chunk in range(csteps):
            for d in range(1, nb):
                ag_copy(d, chunk).start()
        cacc[...] = jnp.zeros_like(cacc)
        cnorm[...] = jnp.zeros_like(cnorm)
        facc[...] = jnp.zeros_like(facc)
        fnorm[...] = jnp.zeros_like(fnorm)
        choice = chooser[...]

        @pl.loop(0, fsteps)
        def _(chunk):
            window = pl.ds(pl.multiple_of(chunk * kf, kf), kf)
            parts = by_part(fine[:, :, window]).astype(BF16)
            chosen = jnp.dot(choice, parts, preferred_element_type=F32)
            for b in range(nb):
                outgoing[b, :, window] = chosen[b * 2 * CAP : (b + 1) * 2 * CAP].astype(BF16)

        slots[me] = outgoing[me]
        for copy in table_copies():
            copy.wait()

    per = fsteps // csteps

    @pl.when(step < csteps)
    def _():
        for p in range(per):
            for d in range(1, nb):
                slot_copy(d, step * per + p).start()
        for d in range(1, nb):
            ag_copy(d, step).wait_recv()
        weight = cweight[...]
        norm_add(
            cnorm,
            lambda r: r // crow,
            lambda r, n, c: (ctemp[0, r : r + n, c : c + 128], ctemp[1, r : r + n, c : c + 128]),
            weight,
            ctemp.shape[1],
            kc,
        )
        base = step * kc
        for c in range(0, kc, sub):
            window = pl.ds(pl.multiple_of(base + c, sub), sub)
            blocks = [ag[b, :, window].astype(F32) for b in range(nb)]
            w = weight[:, c : c + sub]
            real = jnp.concatenate([x[:seg_dev] for x in blocks], axis=0) * w
            imag = jnp.concatenate([x[seg_dev:] for x in blocks], axis=0) * w
            lag_re, lag_im = lag_rows(
                real, imag, cstep[0:1, window], cstep[1:2, window], LC
            )
            left = jnp.concatenate([ctemp[0, :, c : c + sub], ctemp[1, :, c : c + sub]], axis=1)
            re = nt_dot(left, jnp.concatenate([lag_re, lag_im], axis=1))
            im = nt_dot(left, jnp.concatenate([lag_im, -lag_re], axis=1))
            for k in range(nf):
                cacc[k, 0] += re[k * crow : (k + 1) * crow]
                cacc[k, 1] += im[k * crow : (k + 1) * crow]

    @pl.when(step >= csteps)
    def _():
        fs = step - csteps

        @pl.when(fs == min(1, fsteps - 1))
        def _():
            for copy in freq_copies(coarse_pairs, cx_send, cx_recv):
                copy.start()

        for d in range(1, nb):
            slot_copy(d, fs).wait_recv()
        weight = fweight[...]
        norm_add(
            fnorm,
            lambda r: r // q,
            lambda r, n, c: (
                ftemp[0, 0, r : r + n, c : c + 128],
                ftemp[1, 0, r : r + n, c : c + 128],
            ),
            weight,
            ftemp.shape[2],
            kf,
        ) if q % 32 == 0 else norm_small(fnorm, ftemp, weight, nf, q, kf)
        base = fs * kf
        here = lax.broadcasted_iota(jnp.int32, shift_ac.shape, 1) == fs
        ar = jnp.sum(jnp.where(here, shift_ac[...], 0.0), axis=1, keepdims=True)
        ai = jnp.sum(jnp.where(here, shift_as[...], 0.0), axis=1, keepdims=True)
        for c in range(0, kf, fsub):
            window = pl.ds(pl.multiple_of(base + c, fsub), fsub)
            blocks = [slots[b, :, window].astype(F32) for b in range(nb)]
            w = weight[:, c : c + fsub]
            real = jnp.concatenate([x[:CAP] for x in blocks], axis=0) * w
            imag = jnp.concatenate([x[CAP:] for x in blocks], axis=0) * w
            br = shift_bc[:, c : c + fsub]
            bi = shift_bs[:, c : c + fsub]
            sr = ar * br - ai * bi
            si = ar * bi + ai * br
            real, imag = real * sr - imag * si, real * si + imag * sr
            lag_re, lag_im = lag_rows(
                real, imag, fstep[0:1, window], fstep[1:2, window], LF
            )
            both = jnp.concatenate([lag_re, lag_im], axis=0)
            left = jnp.concatenate(
                [ftemp[0, 0, :, c : c + fsub], ftemp[1, 0, :, c : c + fsub]], axis=0
            )
            facc[...] += nt_dot(left, both)

        @pl.when(fs == fsteps - 1)
        def _():
            half = facc.shape[0] // 2
            re = facc[:half, :nfl] + facc[half:, nfl:]
            im = facc[:half, nfl:] - facc[half:, :nfl]
            for k in range(nf):
                fsum[k, 0] = re[k * q : (k + 1) * q]
                fsum[k, 1] = im[k * q : (k + 1) * q]
            fcopies = freq_copies(fine_pairs, fx_send, fx_recv)
            for copy in fcopies:
                copy.start()
            ccopies = freq_copies(coarse_pairs, cx_send, cx_recv)
            for copy in ccopies:
                copy.wait_recv()
            re, im, norm = cacc[fme, 0], cacc[fme, 1], cnorm[fme]
            for d in range(nf - 1):
                re = re + crecv[d, 0]
                im = im + crecv[d, 1]
                norm = norm + cnrecv[d]
            top = peak(re * re + im * im, LC, segs)
            csnr[...] = top[:, :segs] / jnp.sum(norm, axis=1, keepdims=True)
            for copy in fcopies:
                copy.wait_recv()
            re, im, norm = fsum[fme, 0], fsum[fme, 1], fnorm[fme]
            for d in range(nf - 1):
                re = re + frecv[d, 0]
                im = im + frecv[d, 1]
                norm = norm + fnrecv[d]
            top = peak(re * re + im * im, LF, slot_total)
            fsnr[...] = top / jnp.sum(norm, axis=1, keepdims=True)
            back[me] = fsnr[...]
            bcopies = back_copies()
            for copy in bcopies:
                copy.start()
            for copy in ccopies + fcopies:
                copy.wait_send()
            for d in range(1, nb):
                for chunk in range(csteps):
                    ag_copy(d, chunk).wait_send()
                for chunk in range(fsteps):
                    slot_copy(d, chunk).wait_send()
            for copy in bcopies:
                copy.wait()
            rows = None
            for b in range(nb):
                part = lax.dot_general(
                    giver[b],
                    back[b],
                    (((1,), (1,)), ((), ())),
                    precision=lax.Precision.HIGHEST,
                    preferred_element_type=F32,
                )
                rows = part if rows is None else rows + part
            fout[...] = rows


def norm_small(acc, ftemp, weight, nf, q, width):
    for k in range(nf):
        part = jnp.zeros((q, 128), F32)
        for c in range(0, width, 128):
            hr = ftemp[0, 0, k * q : (k + 1) * q, c : c + 128].astype(F32)
            hi = ftemp[1, 0, k * q : (k + 1) * q, c : c + 128].astype(F32)
            part = part + (hr * hr + hi * hi) * weight[:, c : c + 128]
        acc[k] += part


def body(
    coarse_spectra,
    fine_spectra,
    coarse_templates,
    fine_templates,
    coarse_weight,
    fine_weight,
    triggers,
    offsets,
):
    nb = lax.axis_size("bank")
    nf = lax.axis_size("freq")
    bank_self = lax.axis_index("bank")
    freq_self = lax.axis_index("freq")
    seg_local = fine_spectra.shape[0]
    cbins = coarse_spectra.shape[2]
    fbins = fine_spectra.shape[2]
    top_count = triggers.shape[1]
    sub_width = fine_templates.shape[2]
    ctemps = coarse_templates.shape[1]
    slot_total = nb * CAP
    segs = nb * seg_local
    kc = min(1024, cbins)
    kf = min(2048, fbins)
    sub = 512
    fsub = 1024
    csteps = cbins // kc
    fsteps = fbins // kf
    crow = ctemps // nf
    q = sub_width // nf

    trig_blocks = triggers.reshape(nb, seg_local * top_count)
    offset_blocks = offsets.reshape(nb, seg_local * top_count)
    recv_pairs = pair_slots(trig_blocks == bank_self, CAP)
    slot_offsets = jnp.sum(jnp.where(recv_pairs, offset_blocks[:, None, :], 0), axis=2).reshape(-1)
    own_pairs = lax.dynamic_index_in_dim(trig_blocks, bank_self, 0, keepdims=False)
    targets = jnp.arange(nb, dtype=jnp.int32)
    send_pairs = pair_slots(own_pairs[None, :] == targets[:, None], CAP)
    send_segments = jnp.any(send_pairs.reshape(nb, CAP, seg_local, top_count), axis=3)
    chooser = (
        send_segments[:, None, :, None, :] & jnp.eye(2, dtype=bool)[None, :, None, :, None]
    ).astype(BF16)
    pairs = seg_local * top_count
    lanes = jnp.arange(128, dtype=jnp.int32) - bank_self * CAP
    giver = sum(
        jnp.where(send_pairs[:, c, :, None] & (lanes == c)[None, None, :], 1.0, 0.0)
        for c in range(CAP)
    )

    period = 2 * FB
    starts = freq_self * fbins + jnp.arange(fsteps, dtype=jnp.int32) * kf
    shift_ac, shift_as = phase_of(
        offset_count(starts[None, :], slot_offsets[:, None], period), period
    )
    inner = jnp.arange(kf, dtype=jnp.int32)
    shift_bc, shift_bs = phase_of(
        offset_count(inner[None, :], slot_offsets[:, None], period), period
    )
    ctable = jnp.asarray(unit_table(FC, CSTRIDE, 2 * FC))
    ftable = jnp.asarray(unit_table(FB, 1, 2 * FB))

    nc = segs * LC
    nfl = slot_total * LF

    def cblock(i):
        return jnp.minimum(i, csteps - 1)

    def fblock(i):
        return jnp.maximum(i - csteps, 0)

    whole = pl.BlockSpec(memory_space=pltpu.VMEM)
    dma = pltpu.SemaphoreType.DMA
    csnr, fine_rows = pl.pallas_call(
        functools.partial(kernel, (nb, nf, kc, kf, csteps, fsteps, sub, fsub)),
        grid=(csteps + fsteps,),
        out_shape=(
            jax.ShapeDtypeStruct((crow, segs), F32),
            jax.ShapeDtypeStruct((pairs, q), F32),
        ),
        in_specs=[
            whole,
            whole,
            whole,
            whole,
            pl.BlockSpec((2, ctemps, kc), lambda i: (0, 0, cblock(i))),
            pl.BlockSpec((2, 1, sub_width, kf), lambda i: (0, 0, 0, fblock(i))),
            pl.BlockSpec((1, kc), lambda i: (0, cblock(i))),
            pl.BlockSpec((1, kf), lambda i: (0, fblock(i))),
            pl.BlockSpec(memory_space=pl.ANY),
            pl.BlockSpec(memory_space=pl.ANY),
            whole,
            whole,
            whole,
            whole,
        ],
        out_specs=(whole, whole),
        scratch_shapes=[
            pltpu.VMEM((2 * seg_local, cbins), BF16),
            pltpu.VMEM((nb, 2 * CAP, fbins), BF16),
            pltpu.VMEM((2, cbins), F32),
            pltpu.VMEM((2, fbins), F32),
            pltpu.VMEM((q, 128), F32),
            pltpu.VMEM((nb, q, 128), F32),
            pltpu.VMEM((nb, 2 * seg_local, cbins), BF16),
            pltpu.VMEM((nb, 2 * CAP, fbins), BF16),
            pltpu.VMEM((nf, 2, crow, nc), F32),
            pltpu.VMEM((nf, crow, 128), F32),
            pltpu.VMEM((2 * sub_width, 2 * nfl), F32),
            pltpu.VMEM((nf, 2, q, nfl), F32),
            pltpu.VMEM((nf, q, 128), F32),
            pltpu.VMEM((nf - 1, 2, crow, nc), F32),
            pltpu.VMEM((nf - 1, crow, 128), F32),
            pltpu.VMEM((nf - 1, 2, q, nfl), F32),
            pltpu.VMEM((nf - 1, q, 128), F32),
            dma((nb - 1, csteps)),
            dma((nb - 1, csteps)),
            dma((nb - 1, fsteps)),
            dma((nb - 1, fsteps)),
            dma((2,)),
            dma((nf - 1, 2)),
            dma((nf - 1, 2)),
            dma((nf - 1, 2)),
            dma((nf - 1, 2)),
            dma((nb - 1,)),
            dma((nb - 1,)),
        ],
        compiler_params=pltpu.CompilerParams(
            collective_id=0,
            has_side_effects=True,
            dimension_semantics=("arbitrary",),
            vmem_limit_bytes=60 * 1024 * 1024,
        ),
    )(
        coarse_spectra,
        fine_spectra,
        chooser.reshape(nb * 2 * CAP, seg_local * 2),
        giver,
        coarse_templates,
        fine_templates,
        coarse_weight[None, :],
        fine_weight[None, :],
        ctable,
        ftable,
        shift_ac,
        shift_as,
        shift_bc,
        shift_bs,
    )
    fine_snr = fine_rows.reshape(seg_local, top_count, q)
    return (csnr, fine_snr)


def solution(mesh):
    return jax.shard_map(
        body,
        mesh=mesh,
        in_specs=(
            P(("groups", "seg", "bank"), None, "freq"),
            P(("groups", "seg", "bank"), None, "freq"),
            P(None, "bank", "freq"),
            P(None, "bank", None, "freq"),
            P(("groups", "freq")),
            P(("groups", "freq")),
            P(("groups", "seg"), None),
            P(("groups", "seg"), None),
        ),
        out_specs=(
            P(("bank", "freq"), ("groups", "seg")),
            P(("groups", "seg", "bank"), None, "freq"),
        ),
        check_vma=False,
    )
```

profile of v0, /device:TPU:0, one launch (start us, length us, event | category | flops | bytes accessed | tf_op | source)
XLA Modules:
  0.0 66.0 jit_solution(18225408793393812399)
XLA Ops:
  0.7 0.8 %copy.22 = s32[16,2]{1,0:T(8,128)S(1)} copy(s32[16,2]{0,1:T(2,128)} %param.16) | data formatting | bytes 256 | tf_op args[6]
  1.4 0.1 reshape.206
  1.5 0.2 reduce_window_sum.18
  1.7 0.1 eq.122
  1.8 0.1 copy.23
  1.9 0.1 fusion.24
  2.0 0.1 copy.26
  2.1 0.1 copy.24
  2.3 0.1 and_convert_fusion
  2.3 0.7 %reshape.208.chooser = bf16[16,8]{1,0:T(8,128)(2,1)} reshape(bf16[4,2,2,2,4]{4,3,2,1,0:T(2,128)(2,1)S(1)} %and_convert_fusion) | data formatting | bytes 512 | tf_op jit(solution)/shard_map/convert_element_type | solution.py:449
  3.0 0.8 %copy.27 = s32[16,2]{1,0:T(8,128)S(1)} copy(s32[16,2]{0,1:T(2,128)} %param.17) | data formatting | bytes 256 | tf_op args[7]
  3.8 0.1 broadcast_in_dim.48
  3.9 0.1 select_reduce_fusion
  4.0 0.1 copy.28
  4.1 0.1 broadcast_in_dim_reshape.2
  4.2 0.7 %fusion.27 = (f32[8,16]{1,0:T(8,128)}, f32[8,16]{1,0:T(8,128)}) fusion(s32[8]{0:T(128)S(1)} %get-tuple-element.23, s32[8]{0:T(128)S(1)} %get-tuple-element.22, s32[16]{0:T(128)S(1)} %multiply_add_fusion), kind=kLoop, calls=%fused_computation.57 | loop fusion | flops 4992 | bytes 1152 | tf_op jit(solution)/shard_map/sin | solution.py:26
  5.0 0.7 %select_add_fusion.giver = f32[4,8,128]{2,1,0:T(8,128)} fusion(pred[128]{0:T(512)(128)(4,1)S(1)} %get-tuple-element.24, pred[4,8]{1,0:T(4,128)(4,1)S(1)} %get-tuple-element.21, pred[128]{0:T(512)(128)(4,1)S(1)} %get-tuple-element.25, pred[4,8]{1,0:T(4,128)(4,1)S(1)} %get-tuple-element.20), kind=kLoop, calls=%fused_computation.25 | loop fusion | flops 20480 | bytes 16704 | tf_op jit(solution)/shard_map/add | solution.py:452
  5.6 1.1 %fusion.13 = (f32[8,2048]{1,0:T(8,128)}, f32[8,2048]{1,0:T(8,128)}) fusion(s32[8]{0:T(128)S(1)} %get-tuple-element.23, s32[8]{0:T(128)S(1)} %get-tuple-element.22), kind=kLoop, calls=%fused_computation.22 | loop fusion | flops 638976 | bytes 131136 | tf_op jit(solution)/shard_map/sin | solution.py:26
  6.7 56.4 %shard_map.113 = (f32[256,16]{1,0:T(8,128)}, f32[8,32]{1,0:T(8,128)}) custom-call(bf16[4,2,8192]{2,1,0:T(2,128)(2,1)} %coarse.1, bf16[4,2,32768]{2,1,0:T(2,128)(2,1)} %fine.1, bf16[16,8]{1,0:T(8,128)(2,1)} %reshape.208.chooser, f32[4,8,128]{2,1,0:T(8,128)} %select_add_fusion.giver, bf16[2,512,8192]{2,1,0:T(8,128)(2,1)} %ctemp.1, ...), custom_call_target="tpu_custom_call" | custom-call | tf_op jit(solution)/shard_map/pallas_call | solution.py:480
  63.1 1.6 %copy.29 = f32[256,16]{0,1:T(8,128)} copy(f32[256,16]{1,0:T(8,128)} %get-tuple-element.10) | data formatting | bytes 32768
  64.7 1.3 %copy.31 = f32[4,2,32]{2,1,0:T(2,128)} copy(f32[4,2,32]{2,1,0:T(2,128)} %bitcast.15) | data formatting | bytes 2048
  (15 shorter events, 0.2 us)
where the time goes:
time: 66.4 us; the launch traced here: 66 us
  Pallas kernels  56.4 us (85%)
  local copies, waits for them, and re-layouts  5.79 us (9%)
  other arithmetic  3.07 us (5%)
  between operations  0.69 us (1%)
    pallas_call x1, Pallas kernels, body(): pl.pallas_call(functools.partial(kernel, (nb, nf, kc, kf, csteps, fsteps,...  56.4 us
    unnamed x4, local copies, waits for them, and re-layouts  4.37 us
    sin x2, other arithmetic, phase_of(): return (jnp.cos(radians), jnp.sin(radians))  1.79 us

commit v1 on v0

v1 whole, which is shorter than its diff:
```python
import functools
import math

import jax
import jax.numpy as jnp
import numpy as np
from jax import lax
from jax.experimental import pallas as pl
from jax.experimental.pallas import tpu as pltpu
from jax.sharding import PartitionSpec as P

CAP = 2
LC = 16
LF = 16
CSTRIDE = 2047

MESH = pl.DeviceIdType.MESH
F32 = jnp.float32
BF16 = jnp.bfloat16
I32 = jnp.int32


def unit_table(count, stride, period):
    angle = 2.0 * np.pi * ((np.arange(count) * stride) % period) / period
    return np.stack([np.cos(angle), np.sin(angle)]).astype(np.float32)


def nt_dot(left, right):
    return lax.dot_general(left, right, (((1,), (1,)), ((), ())), preferred_element_type=F32)


def lag_series(real, imag, cos, sin, lags, emit):
    emit(0, real, imag)
    prev_re, prev_im = real, imag
    real, imag = real * cos - imag * sin, real * sin + imag * cos
    twice = cos + cos
    for j in range(1, lags):
        emit(j, real, imag)
        if j + 1 < lags:
            next_re = twice * real - prev_re
            next_im = twice * imag - prev_im
            prev_re, prev_im, real, imag = real, imag, next_re, next_im


def peak(energy, width):
    total = energy.shape[1]
    while total > width:
        half = total // 2
        if half % 128 == 0:
            energy = jnp.maximum(energy[:, :half], energy[:, half:])
        else:
            energy = jnp.maximum(energy, pltpu.roll(energy, energy.shape[1] - half, 1))
        total = half
    return energy


def kernel(cfg, *refs):
    nb, nf, kc, kf, chunks, period = cfg
    (
        trig, offs, coarse, fine, ctemp, ftemp, cweight, fweight, ctable, ftable,
        csnr, fout,
        coarse_v, fine_v, ctemp_v, ftemp_v, cw, fw, cstep, fstep,
        ag, outgoing, slots,
        cre0, cim0, cnre0, cre1, cim1, cnre1, fl0, fl1,
        cacc, cnorm, facc, fsum, fnorm, fsnr, back,
        crecv, cnrecv, frecv, fnrecv,
        in_sem, ct_sem, ft_sem,
        agr_send, agr_recv, agl_send, agl_recv, sl_send, sl_recv,
        cx_send, cx_recv, nx_send, nx_recv, fx_send, fx_recv, bk_send, bk_recv,
    ) = refs
    me = lax.axis_index("bank")
    fme = lax.axis_index("freq")
    seg_dev = coarse_v.shape[0]
    segs = nb * seg_dev
    rows = nb * CAP
    cbins = coarse_v.shape[2]
    fbins = fine_v.shape[2]
    csteps = cbins // kc
    fsteps = fbins // kf
    ctemps = ctemp_v.shape[1]
    sub_width = ftemp_v.shape[2]
    crow = ctemps // nf
    q = sub_width // nf
    nc = segs * LC
    nfl = rows * LF
    top_count = trig.shape[0]
    pairs = seg_dev * top_count
    cw_ag = cbins // chunks

    def win(i, width):
        return pl.ds(pl.multiple_of(i * width, width), width)

    small = [
        pltpu.make_async_copy(coarse, coarse_v, in_sem.at[0]),
        pltpu.make_async_copy(fine, fine_v, in_sem.at[1]),
        pltpu.make_async_copy(cweight, cw, in_sem.at[2]),
        pltpu.make_async_copy(fweight, fw, in_sem.at[3]),
        pltpu.make_async_copy(ctable.at[:, win(fme, cbins)], cstep, in_sem.at[4]),
        pltpu.make_async_copy(ftable.at[:, win(fme, fbins)], fstep, in_sem.at[5]),
    ]

    def ct_copy(i):
        return pltpu.make_async_copy(
            ctemp.at[:, :, win(i, kc)], ctemp_v.at[:, :, win(i, kc)], ct_sem.at[i]
        )

    def ft_copy(i):
        return pltpu.make_async_copy(
            ftemp.at[:, :, :, win(i, kf)], ftemp_v.at[:, :, :, win(i, kf)], ft_sem.at[i]
        )

    def ag_right(hop, chunk, block=None):
        block = me - hop if block is None else block
        view = ag.at[block, :, win(chunk, cw_ag)]
        return pltpu.make_async_remote_copy(
            src_ref=view, dst_ref=view,
            send_sem=agr_send.at[hop, chunk], recv_sem=agr_recv.at[hop, chunk],
            device_id={"bank": me + 1}, device_id_type=MESH,
        )

    def ag_left(hop, chunk, block=None):
        block = me + hop if block is None else block
        view = ag.at[block, :, win(chunk, cw_ag)]
        return pltpu.make_async_remote_copy(
            src_ref=view, dst_ref=view,
            send_sem=agl_send.at[hop, chunk], recv_sem=agl_recv.at[hop, chunk],
            device_id={"bank": me - 1}, device_id_type=MESH,
        )

    has_right = me + 1 < nb
    has_left = me >= 1

    def slot_copy(d, step):
        peer = lax.rem(me + d, nb)
        return pltpu.make_async_remote_copy(
            src_ref=outgoing.at[peer, :, win(step, kf)],
            dst_ref=slots.at[me, :, win(step, kf)],
            send_sem=sl_send.at[d - 1, step], recv_sem=sl_recv.at[d - 1, step],
            device_id={"bank": peer}, device_id_type=MESH,
        )

    def freq_copies(pairs_of, send, recv):
        copies = []
        for d in range(1, nf):
            peer = lax.rem(fme + d, nf)
            for k, (source, target) in enumerate(pairs_of):
                copies.append(
                    pltpu.make_async_remote_copy(
                        src_ref=source.at[peer], dst_ref=target.at[d - 1],
                        send_sem=send.at[d - 1, k], recv_sem=recv.at[d - 1, k],
                        device_id={"freq": peer}, device_id_type=MESH,
                    )
                )
        return copies

    def back_copies():
        return [
            pltpu.make_async_remote_copy(
                src_ref=fsnr, dst_ref=back.at[me],
                send_sem=bk_send.at[d - 1], recv_sem=bk_recv.at[d - 1],
                device_id={"bank": lax.rem(me + d, nb)}, device_id_type=MESH,
            )
            for d in range(1, nb)
        ]

    def by_part(block):
        block = block.astype(F32)
        return jnp.concatenate([block[:, 0, :], block[:, 1, :]], axis=0).astype(BF16)

    barrier = pltpu.get_barrier_semaphore()
    for d in range(1, nb):
        pl.semaphore_signal(
            barrier, inc=1, device_id={"bank": lax.rem(me + d, nb)}, device_id_type=MESH
        )
    for d in range(1, nf):
        pl.semaphore_signal(
            barrier, inc=1, device_id={"freq": lax.rem(fme + d, nf)}, device_id_type=MESH
        )
    for copy in small:
        copy.start()
    for i in range(csteps):
        ct_copy(i).start()
    for i in range(fsteps):
        ft_copy(i).start()
    small[0].wait()
    for c in range(chunks):
        ag[me, :, c * cw_ag : (c + 1) * cw_ag] = by_part(
            coarse_v[:, :, c * cw_ag : (c + 1) * cw_ag]
        )
    pl.semaphore_wait(barrier, nb - 1 + nf - 1)
    for c in range(chunks):

        @pl.when(has_right)
        def _():
            ag_right(0, c).start()

        @pl.when(has_left)
        def _():
            ag_left(0, c).start()

    own = [trig[p % top_count, me * seg_dev + p // top_count] for p in range(pairs)]

    def ranks_of(named):
        ranks = []
        for p in range(pairs):
            rank = jnp.int32(0)
            for before in range(p):
                rank = rank + (named[before] == named[p]).astype(I32)
            ranks.append(rank)
        return ranks

    own_rank = ranks_of(own)
    depth = 2 * CAP
    chooser_at = lax.broadcasted_iota(I32, (nb * depth, 2 * seg_dev), 0)
    chosen_col = jnp.zeros_like(chooser_at)
    for b in range(nb):
        for c in range(CAP):
            seg = jnp.int32(0)
            for p in range(pairs):
                hit = (own[p] == b) & (own_rank[p] == c)
                seg = jnp.where(hit, jnp.int32(p // top_count), seg)
            for part in range(2):
                chosen_col = jnp.where(
                    chooser_at == b * depth + part * CAP + c, seg + part * seg_dev, chosen_col
                )
    choice = jnp.where(
        lax.broadcasted_iota(I32, chooser_at.shape, 1) == chosen_col, 1.0, 0.0
    ).astype(BF16)

    small[1].wait()
    group = 2

    @pl.loop(0, fsteps // group)
    def _(i):
        for g in range(group):
            window = win(i * group + g, kf)
            chosen = jnp.dot(
                choice, by_part(fine_v[:, :, window]), preferred_element_type=F32
            ).astype(BF16)
            for b in range(nb):
                outgoing[b, :, window] = chosen[b * depth : (b + 1) * depth]

    slots[me] = outgoing[me]
    for copy in small[2:]:
        copy.wait()

    cnorm[...] = jnp.zeros_like(cnorm)
    fnorm[...] = jnp.zeros_like(fnorm)
    cacc[...] = jnp.zeros_like(cacc)
    facc[...] = jnp.zeros_like(facc)

    def coarse_norm(i):
        ct_copy(i).wait()
        weight = cw[:, win(i, kc)]
        step = 16
        for r in range(0, ctemps, step):
            part = None
            for c in range(0, kc, 128):
                lanes = pl.ds(pl.multiple_of(i * kc + c, 128), 128)
                hr = ctemp_v[0, r : r + step, lanes].astype(F32)
                hi = ctemp_v[1, r : r + step, lanes].astype(F32)
                term = (hr * hr + hi * hi) * weight[:, c : c + 128]
                part = term if part is None else part + term
            cnorm[r // crow, r % crow : r % crow + step, :] += part

    def fine_norm(i):
        ft_copy(i).wait()
        weight = fw[:, win(i, kf)]
        step = 16
        for r in range(0, sub_width, step):
            part = None
            for c in range(0, kf, 128):
                lanes = pl.ds(pl.multiple_of(i * kf + c, 128), 128)
                hr = ftemp_v[0, 0, r : r + step, lanes].astype(F32)
                hi = ftemp_v[1, 0, r : r + step, lanes].astype(F32)
                term = (hr * hr + hi * hi) * weight[:, c : c + 128]
                part = term if part is None else part + term
            fnorm[r // q, r % q : r % q + step, :] += part

    half = csteps // 2
    fillers = [(0, half, coarse_norm), (half, csteps, coarse_norm), (0, fsteps, fine_norm)]
    sent = 0
    for hop in range(nb - 1):
        if hop < len(fillers):
            low, high, fill = fillers[hop]
            pl.loop(low, high)(fill)
        for c in range(chunks):

            @pl.when(me - 1 - hop >= 0)
            def _():
                ag_right(hop, c, me - 1 - hop).wait_recv()

                @pl.when(has_right)
                def _():
                    ag_right(hop + 1, c).start()

            @pl.when(me + 1 + hop < nb)
            def _():
                ag_left(hop, c, me + 1 + hop).wait_recv()

                @pl.when(has_left)
                def _():
                    ag_left(hop + 1, c).start()

        upto = min(fsteps, sent + 2) if hop < nb - 2 else fsteps
        for step in range(sent, upto):
            for d in range(1, nb):
                slot_copy(d, step).start()
        sent = upto
    for low, high, fill in fillers[nb - 1 :]:
        pl.loop(low, high)(fill)
    norm_copies = freq_copies(((cnorm, cnrecv), (fnorm, fnrecv)), nx_send, nx_recv)
    for copy in norm_copies:
        copy.start()

    cbuf = ((cre0, cim0, cnre0), (cre1, cim1, cnre1))

    def coarse_lags(i, buf):
        re_ref, im_ref, nre_ref = buf
        sub = 256
        for c in range(0, kc, sub):
            window = pl.ds(pl.multiple_of(i * kc + c, sub), sub)
            blocks = [ag[b, :, window].astype(F32) for b in range(nb)]
            w = cw[:, window]
            real = jnp.concatenate([x[:seg_dev] for x in blocks], axis=0) * w
            imag = jnp.concatenate([x[seg_dev:] for x in blocks], axis=0) * w

            def emit(j, re, im):
                re = re.astype(BF16)
                re_ref[j * segs : (j + 1) * segs, c : c + sub] = re
                nre_ref[j * segs : (j + 1) * segs, c : c + sub] = -re
                im_ref[j * segs : (j + 1) * segs, c : c + sub] = im.astype(BF16)

            lag_series(real, imag, cstep[0:1, window], cstep[1:2, window], LC, emit)

    def coarse_products(i, buf):
        re_ref, im_ref, nre_ref = buf
        window = win(i, kc)
        left = jnp.concatenate([ctemp_v[0, :, window], ctemp_v[1, :, window]], axis=1)
        re, im, nre = re_ref[...], im_ref[...], nre_ref[...]
        right = jnp.concatenate(
            [jnp.concatenate([re, im], axis=1), jnp.concatenate([im, nre], axis=1)], axis=0
        )
        out = nt_dot(left, right)
        for k in range(nf):
            cacc[k] += out[k * crow : (k + 1) * crow]

    coarse_lags(0, cbuf[0])

    @pl.loop(0, csteps // 2)
    def _(i):
        coarse_lags(2 * i + 1, cbuf[1])
        coarse_products(2 * i, cbuf[0])
        coarse_lags(jnp.minimum(2 * i + 2, csteps - 1), cbuf[0])
        coarse_products(2 * i + 1, cbuf[1])

    coarse_copies = freq_copies(((cacc, crecv),), cx_send, cx_recv)
    for copy in coarse_copies:
        copy.start()

    row_at = lax.broadcasted_iota(I32, (rows, 128), 0)
    shift = jnp.zeros((rows, 128), I32)
    for b in range(nb):
        block = [trig[p % top_count, b * seg_dev + p // top_count] for p in range(pairs)]
        taken = jnp.int32(0)
        for p in range(pairs):
            hit = block[p] == me
            offset = offs[p % top_count, b * seg_dev + p // top_count]
            shift = jnp.where(
                row_at == jnp.where(hit, b * CAP + taken, -1), offset, shift
            )
            taken = taken + hit.astype(I32)
    lane = lax.broadcasted_iota(I32, (rows, 128), 1)
    tiles = fbins // 128
    lane_angle = ((shift * lane) & (period - 1)).astype(F32) * (2.0 * math.pi / period)
    lane_cos, lane_sin = jnp.cos(lane_angle), jnp.sin(lane_angle)
    coarse_period = period // 128
    tile_at = lax.broadcasted_iota(I32, (rows, tiles), 1) + fme * tiles
    wide = jnp.concatenate([shift] * (tiles // 128), axis=1)
    tile_angle = ((wide * tile_at) & (coarse_period - 1)).astype(F32) * (
        2.0 * math.pi / coarse_period
    )
    tile_cos, tile_sin = jnp.cos(tile_angle), jnp.sin(tile_angle)

    def fine_lags(i, buf):
        per = kf // 128
        turn = lax.rem(tiles - i * per, tiles)
        here_cos = pltpu.roll(tile_cos, turn, 1)
        here_sin = pltpu.roll(tile_sin, turn, 1)
        sub = 512
        for c in range(0, kf, sub):
            window = pl.ds(pl.multiple_of(i * kf + c, sub), sub)
            blocks = [slots[b, :, window].astype(F32) for b in range(nb)]
            w = fw[:, window]
            real = jnp.concatenate([x[:CAP] for x in blocks], axis=0) * w
            imag = jnp.concatenate([x[CAP:] for x in blocks], axis=0) * w
            turn_re, turn_im = [], []
            for t in range(c // 128, (c + sub) // 128):
                a_cos = here_cos[:, t : t + 1]
                a_sin = here_sin[:, t : t + 1]
                turn_re.append(a_cos * lane_cos - a_sin * lane_sin)
                turn_im.append(a_cos * lane_sin + a_sin * lane_cos)
            sr = jnp.concatenate(turn_re, axis=1)
            si = jnp.concatenate(turn_im, axis=1)
            real, imag = real * sr - imag * si, real * si + imag * sr
            held = []

            def emit(j, re, im):
                held.append((re, im))
                if len(held) == 2:
                    low, high = (j - 1) * rows, (j + 1) * rows
                    buf[low:high, c : c + sub] = jnp.concatenate(
                        [held[0][0], held[1][0]], axis=0
                    ).astype(BF16)
                    buf[nfl + low : nfl + high, c : c + sub] = jnp.concatenate(
                        [held[0][1], held[1][1]], axis=0
                    ).astype(BF16)
                    held.clear()

            lag_series(real, imag, fstep[0:1, window], fstep[1:2, window], LF, emit)

    def fine_products(i, buf):
        window = win(i, kf)
        left = jnp.concatenate([ftemp_v[0, 0, :, window], ftemp_v[1, 0, :, window]], axis=0)
        facc[...] += nt_dot(left, buf[...])

    def slots_here(step):
        for d in range(1, nb):
            slot_copy(d, step).wait_recv()

    slots_here(0)
    fine_lags(0, fl0)

    @pl.loop(0, fsteps // 2 - 1)
    def _(i):
        slots_here(2 * i + 1)
        slots_here(2 * i + 2)
        fine_lags(2 * i + 1, fl1)
        fine_products(2 * i, fl0)
        fine_lags(2 * i + 2, fl0)
        fine_products(2 * i + 1, fl1)

    slots_here(fsteps - 1)
    fine_lags(fsteps - 1, fl1)
    fine_products(fsteps - 2, fl0)
    fine_products(fsteps - 1, fl1)

    both = facc.shape[0] // 2
    re = facc[:both, :nfl] + facc[both:, nfl:]
    im = facc[:both, nfl:] - facc[both:, :nfl]
    for k in range(nf):
        fsum[k, 0] = re[k * q : (k + 1) * q]
        fsum[k, 1] = im[k * q : (k + 1) * q]
    fine_copies = freq_copies(((fsum, frecv),), fx_send, fx_recv)
    for copy in fine_copies:
        copy.start()
    for copy in norm_copies + fine_copies:
        copy.wait_recv()
    re, im, norm = fsum[fme, 0], fsum[fme, 1], fnorm[fme]
    for d in range(nf - 1):
        re = re + frecv[d, 0]
        im = im + frecv[d, 1]
        norm = norm + fnrecv[d]
    top = peak(re * re + im * im, rows)[:, :128]
    fsnr[...] = top / jnp.sum(norm, axis=1, keepdims=True)
    bcopies = back_copies()
    for copy in bcopies:
        copy.start()
    back[me] = fsnr[...]

    for copy in coarse_copies:
        copy.wait_recv()
    acc, norm = cacc[fme], cnorm[fme]
    for d in range(nf - 1):
        acc = acc + crecv[d]
        norm = norm + cnrecv[d]
    re, im = acc[:, :nc], acc[:, nc:]
    top = peak(re * re + im * im, segs)
    csnr[...] = jnp.transpose(top[:, :128] / jnp.sum(norm, axis=1, keepdims=True))[:segs]

    for copy in coarse_copies + norm_copies + fine_copies:
        copy.wait_send()
    for hop in range(nb - 1):
        for c in range(chunks):

            @pl.when(has_right & (me - hop >= 0))
            def _():
                ag_right(hop, c).wait_send()

            @pl.when(has_left & (me + hop < nb))
            def _():
                ag_left(hop, c).wait_send()

    @pl.loop(0, fsteps)
    def _(step):
        for d in range(1, nb):
            slot_copy(d, step).wait_send()

    for copy in bcopies:
        copy.wait()
    at = lax.broadcasted_iota(I32, back.shape[1:], 1)
    gathered = jnp.zeros(back.shape[1:], F32)
    for b in range(nb):
        turned = pltpu.roll(back[b], lax.rem((b - me + nb) * CAP + 128 - nb * CAP, 128), 1)
        gathered = jnp.where((at >= b * CAP) & (at < (b + 1) * CAP), turned, gathered)
    pair_at = lax.broadcasted_iota(I32, (pairs, 128), 0)
    place = jnp.zeros((pairs, 128), I32)
    for p in range(pairs):
        place = jnp.where(pair_at == p, own[p] * CAP + own_rank[p], place)
    giver = jnp.where(lax.broadcasted_iota(I32, (pairs, 128), 1) == place, 1.0, 0.0)
    fout[...] = lax.dot_general(
        giver, gathered, (((1,), (1,)), ((), ())),
        precision=lax.Precision.HIGHEST, preferred_element_type=F32,
    )


def body(
    coarse_spectra,
    fine_spectra,
    coarse_templates,
    fine_templates,
    coarse_weight,
    fine_weight,
    triggers,
    offsets,
):
    nb = lax.axis_size("bank")
    nf = lax.axis_size("freq")
    seg_local = fine_spectra.shape[0]
    cbins = coarse_spectra.shape[2]
    fbins = fine_spectra.shape[2]
    top_count = triggers.shape[1]
    sub_width = fine_templates.shape[2]
    ctemps = coarse_templates.shape[1]
    rows = nb * CAP
    segs = nb * seg_local
    kc = min(1024, cbins // 2)
    kf = min(2048, fbins // 2)
    chunks = 4
    csteps = cbins // kc
    fsteps = fbins // kf
    crow = ctemps // nf
    q = sub_width // nf
    period = 2 * fbins * nf
    assert period & (period - 1) == 0 and csteps % 2 == 0 and fsteps % 2 == 0
    nc = segs * LC
    nfl = rows * LF
    ctable = jnp.asarray(unit_table(cbins * nf, CSTRIDE, 2 * cbins * nf))
    ftable = jnp.asarray(unit_table(fbins * nf, 1, period))

    vmem, anywhere, scalar = (
        pl.BlockSpec(memory_space=pltpu.VMEM),
        pl.BlockSpec(memory_space=pl.ANY),
        pl.BlockSpec(memory_space=pltpu.SMEM),
    )
    dma = pltpu.SemaphoreType.DMA
    lag_buf = pltpu.VMEM((nc, kc), BF16)
    fine_buf = pltpu.VMEM((2 * nfl, kf), BF16)
    csnr, fine_rows = pl.pallas_call(
        functools.partial(kernel, (nb, nf, kc, kf, chunks, period)),
        out_shape=(
            jax.ShapeDtypeStruct((segs, crow), F32),
            jax.ShapeDtypeStruct((seg_local * top_count, q), F32),
        ),
        in_specs=[scalar, scalar] + [anywhere] * 8,
        out_specs=(vmem, vmem),
        scratch_shapes=[
            pltpu.VMEM(coarse_spectra.shape, BF16),
            pltpu.VMEM(fine_spectra.shape, BF16),
            pltpu.VMEM(coarse_templates.shape, BF16),
            pltpu.VMEM(fine_templates.shape, BF16),
            pltpu.VMEM((1, cbins), F32),
            pltpu.VMEM((1, fbins), F32),
            pltpu.VMEM((2, cbins), F32),
            pltpu.VMEM((2, fbins), F32),
            pltpu.VMEM((nb, 2 * seg_local, cbins), BF16),
            pltpu.VMEM((nb, 2 * CAP, fbins), BF16),
            pltpu.VMEM((nb, 2 * CAP, fbins), BF16),
            lag_buf, lag_buf, lag_buf, lag_buf, lag_buf, lag_buf,
            fine_buf, fine_buf,
            pltpu.VMEM((nf, crow, 2 * nc), F32),
            pltpu.VMEM((nf, crow, 128), F32),
            pltpu.VMEM((2 * sub_width, 2 * nfl), F32),
            pltpu.VMEM((nf, 2, q, nfl), F32),
            pltpu.VMEM((nf, q, 128), F32),
            pltpu.VMEM((q, 128), F32),
            pltpu.VMEM((nb, q, 128), F32),
            pltpu.VMEM((nf - 1, crow, 2 * nc), F32),
            pltpu.VMEM((nf - 1, crow, 128), F32),
            pltpu.VMEM((nf - 1, 2, q, nfl), F32),
            pltpu.VMEM((nf - 1, q, 128), F32),
            dma((6,)),
            dma((csteps,)),
            dma((fsteps,)),
            dma((nb - 1, chunks)),
            dma((nb - 1, chunks)),
            dma((nb - 1, chunks)),
            dma((nb - 1, chunks)),
            dma((nb - 1, fsteps)),
            dma((nb - 1, fsteps)),
            dma((nf - 1, 1)),
            dma((nf - 1, 1)),
            dma((nf - 1, 2)),
            dma((nf - 1, 2)),
            dma((nf - 1, 1)),
            dma((nf - 1, 1)),
            dma((nb - 1,)),
            dma((nb - 1,)),
        ],
        compiler_params=pltpu.CompilerParams(
            collective_id=0,
            has_side_effects=True,
            vmem_limit_bytes=60 * 1024 * 1024,
        ),
    )(
        triggers.T,
        offsets.T,
        coarse_spectra,
        fine_spectra,
        coarse_templates,
        fine_templates,
        coarse_weight[None, :],
        fine_weight[None, :],
        ctable,
        ftable,
    )
    return (csnr.T, fine_rows.reshape(seg_local, top_count, q))


def solution(mesh):
    return jax.shard_map(
        body,
        mesh=mesh,
        in_specs=(
            P(("groups", "seg", "bank"), None, "freq"),
            P(("groups", "seg", "bank"), None, "freq"),
            P(None, "bank", "freq"),
            P(None, "bank", None, "freq"),
            P(("groups", "freq")),
            P(("groups", "freq")),
            P(("groups", "seg"), None),
            P(("groups", "seg"), None),
        ),
        out_specs=(
            P(("bank", "freq"), ("groups", "seg")),
            P(("groups", "seg", "bank"), None, "freq"),
        ),
        check_vma=False,
    )
```

time: 66.4 us -> 58 us (0.87)
  local copies, waits for them, and re-layouts: 5.79 us -> 2.59 us
  other arithmetic: 3.07 us -> 0 us
  Pallas kernels: 56.4 us -> 54.4 us
    pallas_call x1, Pallas kernels: 56.4 us -> 54.4 us  [body(): pl.pallas_call(functools.partial(kernel, (nb, nf, kc, kf, chunks, period)...]
    sin x2 -> x0, other arithmetic: 1.79 us -> none  [phase_of(): return (jnp.cos(radians), jnp.sin(radians))]
    unnamed x4 -> x2, local copies, waits for them, and re-layouts: 4.37 us -> 2.59 us
    add x2 -> x0, other arithmetic: 0.69 us -> none  [the longest x1 0.68 us: body(): sum((jnp.where(send_pairs[:, c, :, None] & (lanes == c)[None, None, :], 1...]
    convert_element_type x1 -> x0, local copies, waits for them, and re-layouts: 0.68 us -> none  [body(): chooser = (send_segments[:, None, :, None, :] & jnp.eye(2, dtype=bool)[No...]
where the time goes in v1:
time: 58 us; the launch traced here: 57.7 us
  Pallas kernels  54.4 us (94%)
  local copies, waits for them, and re-layouts  2.59 us (4%)
  between operations  0.64 us (1%)
    pallas_call x1, Pallas kernels, body(): pl.pallas_call(functools.partial(kernel, (nb, nf, kc, kf, chunks, period)...  54.4 us
    unnamed x2, local copies, waits for them, and re-layouts  2.59 us

profile of v1, /device:TPU:0, one launch (start us, length us, event | category | flops | bytes accessed | tf_op | source)
XLA Modules:
  0.0 57.7 jit_solution(12231035139330462879)
XLA Ops:
  0.6 54.4 %shard_map.113 = (f32[16,256]{1,0:T(8,128)}, f32[8,32]{1,0:T(8,128)}) custom-call(s32[2,16]{1,0:T(2,128)} %bitcast.10, s32[2,16]{1,0:T(2,128)} %bitcast.11, bf16[4,2,8192]{2,1,0:T(2,128)(2,1)} %refs_2_.1, bf16[4,2,32768]{2,1,0:T(2,128)(2,1)} %refs_3_.1, bf16[2,512,8192]{2,1,0:T(8,128)(2,1)} %refs_4_.1, bf16[2,1,64,32768]{3,2,1,0:T(8,128)(2,1)} %refs_5_.1, ...), custom_call_target="tpu_custom_call" | custom-call | tf_op jit(solution)/shard_map/pallas_call | solution.py:559
  55.1 1.3 %copy.14 = f32[256,16]{0,1:T(8,128)} copy(f32[256,16]{0,1:T(8,128)} %bitcast.8) | data formatting | bytes 32768
  56.4 1.3 %copy.15 = f32[4,2,32]{2,1,0:T(2,128)} copy(f32[4,2,32]{2,1,0:T(2,128)} %bitcast.9) | data formatting | bytes 2048

commit v2 on v1

--- a/solution.py
+++ b/solution.py
@@ -55,21 +55,22 @@
 
 
 def kernel(cfg, *refs):
-    nb, nf, kc, kf, chunks, period = cfg
+    nb, nf, ns, fsplit, kc, kf, chunks, period = cfg
     (
-        trig, offs, coarse, fine, ctemp, ftemp, cweight, fweight, ctable, ftable,
+        trig_h, offs_h, coarse, fine, ctemp, ftemp, cweight, fweight, ctable, ftable,
         csnr, fout,
-        coarse_v, fine_v, ctemp_v, ftemp_v, cw, fw, cstep, fstep,
+        trig, offs, coarse_v, fine_v, ctemp_v, ftemp_v, cw, fw, cstep, fstep,
         ag, outgoing, slots,
         cre0, cim0, cnre0, cre1, cim1, cnre1, fl0, fl1,
-        cacc, cnorm, facc, fsum, fnorm, fsnr, back,
-        crecv, cnrecv, frecv, fnrecv,
+        cacc, cnorm, cnall, facc, fsum, fnorm, fnall, fsnr, back,
+        crecv, frecv,
         in_sem, ct_sem, ft_sem,
         agr_send, agr_recv, agl_send, agl_recv, sl_send, sl_recv,
         cx_send, cx_recv, nx_send, nx_recv, fx_send, fx_recv, bk_send, bk_recv,
     ) = refs
     me = lax.axis_index("bank")
     fme = lax.axis_index("freq")
+    sme = lax.axis_index("seg")
     seg_dev = coarse_v.shape[0]
     segs = nb * seg_dev
     rows = nb * CAP
@@ -81,6 +82,7 @@
     sub_width = ftemp_v.shape[2]
     crow = ctemps // nf
     q = sub_width // nf
+    fshare = q // fsplit
     nc = segs * LC
     nfl = rows * LF
     top_count = trig.shape[0]
@@ -92,6 +94,8 @@
 
     small = [
         pltpu.make_async_copy(coarse, coarse_v, in_sem.at[0]),
+        pltpu.make_async_copy(trig_h, trig, in_sem.at[6]),
+        pltpu.make_async_copy(offs_h, offs, in_sem.at[7]),
         pltpu.make_async_copy(fine, fine_v, in_sem.at[1]),
         pltpu.make_async_copy(cweight, cw, in_sem.at[2]),
         pltpu.make_async_copy(fweight, fw, in_sem.at[3]),
@@ -172,22 +176,23 @@
         pl.semaphore_signal(
             barrier, inc=1, device_id={"bank": lax.rem(me + d, nb)}, device_id_type=MESH
         )
-    for d in range(1, nf):
+    for d in range(1, nf * ns):
+        x, s = lax.rem(fme + d // ns, nf), lax.rem(sme + d % ns, ns)
         pl.semaphore_signal(
-            barrier, inc=1, device_id={"freq": lax.rem(fme + d, nf)}, device_id_type=MESH
+            barrier, inc=1, device_id={"freq": x, "seg": s}, device_id_type=MESH
         )
     for copy in small:
         copy.start()
     for i in range(csteps):
-        ct_copy(i).start()
-    for i in range(fsteps):
-        ft_copy(i).start()
+        ct_copy(i).start(priority=1)
+        for k in range(i * fsteps // csteps, (i + 1) * fsteps // csteps):
+            ft_copy(k).start(priority=1)
     small[0].wait()
     for c in range(chunks):
         ag[me, :, c * cw_ag : (c + 1) * cw_ag] = by_part(
             coarse_v[:, :, c * cw_ag : (c + 1) * cw_ag]
         )
-    pl.semaphore_wait(barrier, nb - 1 + nf - 1)
+    pl.semaphore_wait(barrier, nb - 1 + nf * ns - 1)
     for c in range(chunks):
 
         @pl.when(has_right)
@@ -198,6 +203,7 @@
         def _():
             ag_left(0, c).start()
 
+    small[1].wait()
     own = [trig[p % top_count, me * seg_dev + p // top_count] for p in range(pairs)]
 
     def ranks_of(named):
@@ -227,7 +233,7 @@
         lax.broadcasted_iota(I32, chooser_at.shape, 1) == chosen_col, 1.0, 0.0
     ).astype(BF16)
 
-    small[1].wait()
+    small[3].wait()
     group = 2
 
     @pl.loop(0, fsteps // group)
@@ -241,7 +247,7 @@
                 outgoing[b, :, window] = chosen[b * depth : (b + 1) * depth]
 
     slots[me] = outgoing[me]
-    for copy in small[2:]:
+    for copy in small[2:3] + small[4:]:
         copy.wait()
 
     cnorm[...] = jnp.zeros_like(cnorm)
@@ -249,69 +255,128 @@
     cacc[...] = jnp.zeros_like(cacc)
     facc[...] = jnp.zeros_like(facc)
 
+    cshare = crow // ns
+
+    def norm_rows(acc, k, place, temps, start, bins, width, weight):
+        part = None
+        rows_at = pl.ds(pl.multiple_of(start, 16), 16)
+        for c in range(0, width, 128):
+            lanes = pl.ds(pl.multiple_of(bins + c, 128), 128)
+            hr, hi = temps(rows_at, lanes)
+            hr, hi = hr.astype(F32), hi.astype(F32)
+            term = (hr * hr + hi * hi) * weight[:, c : c + 128]
+            part = term if part is None else part + term
+        acc[k, place : place + 16, :] += part
+
     def coarse_norm(i):
         ct_copy(i).wait()
         weight = cw[:, win(i, kc)]
-        step = 16
-        for r in range(0, ctemps, step):
-            part = None
-            for c in range(0, kc, 128):
-                lanes = pl.ds(pl.multiple_of(i * kc + c, 128), 128)
-                hr = ctemp_v[0, r : r + step, lanes].astype(F32)
-                hi = ctemp_v[1, r : r + step, lanes].astype(F32)
-                term = (hr * hr + hi * hi) * weight[:, c : c + 128]
-                part = term if part is None else part + term
-            cnorm[r // crow, r % crow : r % crow + step, :] += part
+        for k in range(nf):
+            for r in range(0, cshare, 16):
+                norm_rows(
+                    cnorm, k, r,
+                    lambda rows_at, lanes: (ctemp_v[0, rows_at, lanes], ctemp_v[1, rows_at, lanes]),
+                    k * crow + sme * cshare + r, i * kc, kc, weight,
+                )
 
     def fine_norm(i):
         ft_copy(i).wait()
         weight = fw[:, win(i, kf)]
-        step = 16
-        for r in range(0, sub_width, step):
-            part = None
-            for c in range(0, kf, 128):
-                lanes = pl.ds(pl.multiple_of(i * kf + c, 128), 128)
-                hr = ftemp_v[0, 0, r : r + step, lanes].astype(F32)
-                hi = ftemp_v[1, 0, r : r + step, lanes].astype(F32)
-                term = (hr * hr + hi * hi) * weight[:, c : c + 128]
-                part = term if part is None else part + term
-            fnorm[r // q, r % q : r % q + step, :] += part
-
-    half = csteps // 2
-    fillers = [(0, half, coarse_norm), (half, csteps, coarse_norm), (0, fsteps, fine_norm)]
-    sent = 0
-    for hop in range(nb - 1):
-        if hop < len(fillers):
-            low, high, fill = fillers[hop]
-            pl.loop(low, high)(fill)
-        for c in range(chunks):
-
-            @pl.when(me - 1 - hop >= 0)
+        for k in range(nf):
+            for r in range(0, fshare, 16):
+                norm_rows(
+                    fnorm, k, r,
+                    lambda rows_at, lanes: (
+                        ftemp_v[0, 0, rows_at, lanes], ftemp_v[1, 0, rows_at, lanes],
+                    ),
+                    k * q + (sme * fshare if fsplit > 1 else 0) + r, i * kf, kf, weight,
+                )
+
+    def slots_off(rightward):
+        for dist in range(1, nb):
+            there = me + dist < nb if rightward else me >= dist
+
+            @pl.when(there)
             def _():
-                ag_right(hop, c, me - 1 - hop).wait_recv()
-
-                @pl.when(has_right)
-                def _():
-                    ag_right(hop + 1, c).start()
-
-            @pl.when(me + 1 + hop < nb)
+                @pl.loop(0, fsteps)
+                def _(step):
+                    slot_copy(dist if rightward else nb - dist, step).start()
+
+    def gathered_chunk(hop, c):
+        @pl.when(me - 1 - hop >= 0)
+        def _():
+            ag_right(hop, c, me - 1 - hop).wait_recv()
+
+            @pl.when(has_right)
             def _():
-                ag_left(hop, c, me + 1 + hop).wait_recv()
-
-                @pl.when(has_left)
-                def _():
-                    ag_left(hop + 1, c).start()
-
-        upto = min(fsteps, sent + 2) if hop < nb - 2 else fsteps
-        for step in range(sent, upto):
-            for d in range(1, nb):
-                slot_copy(d, step).start()
-        sent = upto
-    for low, high, fill in fillers[nb - 1 :]:
-        pl.loop(low, high)(fill)
-    norm_copies = freq_copies(((cnorm, cnrecv), (fnorm, fnrecv)), nx_send, nx_recv)
+                ag_right(hop + 1, c).start()
+
+        @pl.when(me + 1 + hop < nb)
+        def _():
+            ag_left(hop, c, me + 1 + hop).wait_recv()
+
+            @pl.when(has_left)
+            def _():
+                ag_left(hop + 1, c).start()
+
+        if c == chunks - 1:
+
+            @pl.when(me == hop + 1)
+            def _():
+                slots_off(True)
+
+            @pl.when(nb - 1 - me == hop + 1)
+            def _():
+                slots_off(False)
+
+    @pl.when(me == 0)
+    def _():
+        slots_off(True)
+
+    @pl.when(me == nb - 1)
+    def _():
+        slots_off(False)
+
+    events = [(hop, c) for hop in range(nb - 1) for c in range(chunks)]
+    per = fsteps // csteps
+    first = 2 * csteps // 8
+
+    @pl.loop(0, csteps)
+    def _(i):
+        coarse_norm(i)
+        for at in range(first, csteps):
+
+            @pl.when(i == at)
+            def _():
+                gathered_chunk(*events[at - first])
+
+        for k in range(per):
+            fine_norm(i * per + k)
+
+    cnall[fme, sme] = cnorm[fme]
+    fnall[fme, sme if fsplit > 1 else 0] = fnorm[fme]
+    norm_copies = []
+    for dx in range(nf):
+        for ds in range(ns):
+            if dx + ds == 0:
+                continue
+            x, s = lax.rem(fme + dx, nf), lax.rem(sme + ds, ns)
+            kinds = [(cnorm, cnall, sme)]
+            if fsplit > 1 or ds == 0:
+                kinds.append((fnorm, fnall, sme if fsplit > 1 else 0))
+            for kind, (source, target, at) in enumerate(kinds):
+                norm_copies.append(
+                    pltpu.make_async_remote_copy(
+                        src_ref=source.at[x], dst_ref=target.at[fme, at],
+                        send_sem=nx_send.at[dx * ns + ds, kind],
+                        recv_sem=nx_recv.at[dx * ns + ds, kind],
+                        device_id={"freq": x, "seg": s}, device_id_type=MESH,
+                    )
+                )
     for copy in norm_copies:
         copy.start()
+    for event in events[csteps - first :]:
+        gathered_chunk(*event)
 
     cbuf = ((cre0, cim0, cnre0), (cre1, cim1, cnre1))
 
@@ -456,13 +521,21 @@
         copy.start()
     for copy in norm_copies + fine_copies:
         copy.wait_recv()
-    re, im, norm = fsum[fme, 0], fsum[fme, 1], fnorm[fme]
+    def whole_norm(parts):
+        shares = []
+        for s in range(parts.shape[1]):
+            total = parts[0, s]
+            for x in range(1, nf):
+                total = total + parts[x, s]
+            shares.append(total)
+        return jnp.sum(jnp.concatenate(shares, axis=0), axis=1, keepdims=True)
+
+    re, im = fsum[fme, 0], fsum[fme, 1]
     for d in range(nf - 1):
         re = re + frecv[d, 0]
         im = im + frecv[d, 1]
-        norm = norm + fnrecv[d]
     top = peak(re * re + im * im, rows)[:, :128]
-    fsnr[...] = top / jnp.sum(norm, axis=1, keepdims=True)
+    fsnr[...] = top / whole_norm(fnall)
     bcopies = back_copies()
     for copy in bcopies:
         copy.start()
@@ -470,13 +543,12 @@
 
     for copy in coarse_copies:
         copy.wait_recv()
-    acc, norm = cacc[fme], cnorm[fme]
+    acc = cacc[fme]
     for d in range(nf - 1):
         acc = acc + crecv[d]
-        norm = norm + cnrecv[d]
     re, im = acc[:, :nc], acc[:, nc:]
     top = peak(re * re + im * im, segs)
-    csnr[...] = jnp.transpose(top[:, :128] / jnp.sum(norm, axis=1, keepdims=True))[:segs]
+    csnr[...] = jnp.transpose(top[:, :128] / whole_norm(cnall))[:segs]
 
     for copy in coarse_copies + norm_copies + fine_copies:
         copy.wait_send()
@@ -526,6 +598,7 @@
 ):
     nb = lax.axis_size("bank")
     nf = lax.axis_size("freq")
+    ns = lax.axis_size("seg")
     seg_local = fine_spectra.shape[0]
     cbins = coarse_spectra.shape[2]
     fbins = fine_spectra.shape[2]
@@ -542,29 +615,28 @@
     crow = ctemps // nf
     q = sub_width // nf
     period = 2 * fbins * nf
+    fsplit = ns if q // ns % 16 == 0 else 1
     assert period & (period - 1) == 0 and csteps % 2 == 0 and fsteps % 2 == 0
     nc = segs * LC
     nfl = rows * LF
     ctable = jnp.asarray(unit_table(cbins * nf, CSTRIDE, 2 * cbins * nf))
     ftable = jnp.asarray(unit_table(fbins * nf, 1, period))
 
-    vmem, anywhere, scalar = (
-        pl.BlockSpec(memory_space=pltpu.VMEM),
-        pl.BlockSpec(memory_space=pl.ANY),
-        pl.BlockSpec(memory_space=pltpu.SMEM),
-    )
+    vmem, anywhere = pl.BlockSpec(memory_space=pltpu.VMEM), pl.BlockSpec(memory_space=pl.ANY)
     dma = pltpu.SemaphoreType.DMA
     lag_buf = pltpu.VMEM((nc, kc), BF16)
     fine_buf = pltpu.VMEM((2 * nfl, kf), BF16)
     csnr, fine_rows = pl.pallas_call(
-        functools.partial(kernel, (nb, nf, kc, kf, chunks, period)),
+        functools.partial(kernel, (nb, nf, ns, fsplit, kc, kf, chunks, period)),
         out_shape=(
             jax.ShapeDtypeStruct((segs, crow), F32),
             jax.ShapeDtypeStruct((seg_local * top_count, q), F32),
         ),
-        in_specs=[scalar, scalar] + [anywhere] * 8,
+        in_specs=[anywhere] * 10,
         out_specs=(vmem, vmem),
         scratch_shapes=[
+            pltpu.SMEM((top_count, triggers.shape[0]), I32),
+            pltpu.SMEM((top_count, triggers.shape[0]), I32),
             pltpu.VMEM(coarse_spectra.shape, BF16),
             pltpu.VMEM(fine_spectra.shape, BF16),
             pltpu.VMEM(coarse_templates.shape, BF16),
@@ -579,17 +651,17 @@
             lag_buf, lag_buf, lag_buf, lag_buf, lag_buf, lag_buf,
             fine_buf, fine_buf,
             pltpu.VMEM((nf, crow, 2 * nc), F32),
-            pltpu.VMEM((nf, crow, 128), F32),
+            pltpu.VMEM((nf, crow // ns, 128), F32),
+            pltpu.VMEM((nf, ns, crow // ns, 128), F32),
             pltpu.VMEM((2 * sub_width, 2 * nfl), F32),
             pltpu.VMEM((nf, 2, q, nfl), F32),
-            pltpu.VMEM((nf, q, 128), F32),
+            pltpu.VMEM((nf, q // fsplit, 128), F32),
+            pltpu.VMEM((nf, fsplit, q // fsplit, 128), F32),
             pltpu.VMEM((q, 128), F32),
             pltpu.VMEM((nb, q, 128), F32),
             pltpu.VMEM((nf - 1, crow, 2 * nc), F32),
-            pltpu.VMEM((nf - 1, crow, 128), F32),
             pltpu.VMEM((nf - 1, 2, q, nfl), F32),
-            pltpu.VMEM((nf - 1, q, 128), F32),
-            dma((6,)),
+            dma((8,)),
             dma((csteps,)),
             dma((fsteps,)),
             dma((nb - 1, chunks)),
@@ -600,8 +672,8 @@
             dma((nb - 1, fsteps)),
             dma((nf - 1, 1)),
             dma((nf - 1, 1)),
-            dma((nf - 1, 2)),
-            dma((nf - 1, 2)),
+            dma((nf * ns, 2)),
+            dma((nf * ns, 2)),
             dma((nf - 1, 1)),
             dma((nf - 1, 1)),
             dma((nb - 1,)),

time: 58 us -> 54 us (0.931)
  Pallas kernels: 54.4 us -> 50.5 us
    pallas_call x1, Pallas kernels: 54.4 us -> 50.5 us  [body(): pl.pallas_call(functools.partial(kernel, (nb, nf, ns, fsplit, kc, kf, chu...]
where the time goes in v2:
time: 54 us; the launch traced here: 53.7 us
  Pallas kernels  50.5 us (94%)
  local copies, waits for them, and re-layouts  2.59 us (5%)
  between operations  0.64 us (1%)
    pallas_call x1, Pallas kernels, body(): pl.pallas_call(functools.partial(kernel, (nb, nf, ns, fsplit, kc, kf, chu...  50.5 us
    unnamed x2, local copies, waits for them, and re-layouts  2.59 us

profile of v2, /device:TPU:0, one launch (start us, length us, event | category | flops | bytes accessed | tf_op | source)
XLA Modules:
  0.0 53.7 jit_solution(9848856421386070376)
XLA Ops:
  0.6 50.5 %shard_map.113 = (f32[16,256]{1,0:T(8,128)}, f32[8,32]{1,0:T(8,128)}) custom-call(s32[2,16]{1,0:T(2,128)} %bitcast.10, s32[2,16]{1,0:T(2,128)} %bitcast.11, bf16[4,2,8192]{2,1,0:T(2,128)(2,1)} %refs_2_.1, bf16[4,2,32768]{2,1,0:T(2,128)(2,1)} %refs_3_.1, bf16[2,512,8192]{2,1,0:T(8,128)(2,1)} %refs_4_.1, bf16[2,1,64,32768]{3,2,1,0:T(8,128)(2,1)} %refs_5_.1, ...), custom_call_target="tpu_custom_call" | custom-call | tf_op jit(solution)/shard_map/pallas_call | solution.py:629
  51.1 1.3 %copy.14 = f32[256,16]{0,1:T(8,128)} copy(f32[256,16]{0,1:T(8,128)} %bitcast.8) | data formatting | bytes 32768
  52.5 1.3 %copy.15 = f32[4,2,32]{2,1,0:T(2,128)} copy(f32[4,2,32]{2,1,0:T(2,128)} %bitcast.9) | data formatting | bytes 2048

commit v3 on v2

--- a/solution.py
+++ b/solution.py
@@ -63,7 +63,7 @@
         ag, outgoing, slots,
         cre0, cim0, cnre0, cre1, cim1, cnre1, fl0, fl1,
         cacc, cnorm, cnall, facc, fsum, fnorm, fnall, fsnr, back,
-        crecv, frecv,
+        csend, crecv, frecv,
         in_sem, ct_sem, ft_sem,
         agr_send, agr_recv, agl_send, agl_recv, sl_send, sl_recv,
         cx_send, cx_recv, nx_send, nx_recv, fx_send, fx_recv, bk_send, bk_recv,
@@ -134,14 +134,23 @@
     has_right = me + 1 < nb
     has_left = me >= 1
 
-    def slot_copy(d, step):
+    couples = fsteps // 2 - 1
+
+    def slot_copy(d, place, start, width):
         peer = lax.rem(me + d, nb)
+        window = pl.ds(pl.multiple_of(start, kf), width)
         return pltpu.make_async_remote_copy(
-            src_ref=outgoing.at[peer, :, win(step, kf)],
-            dst_ref=slots.at[me, :, win(step, kf)],
-            send_sem=sl_send.at[d - 1, step], recv_sem=sl_recv.at[d - 1, step],
+            src_ref=outgoing.at[peer, :, window],
+            dst_ref=slots.at[me, :, window],
+            send_sem=sl_send.at[d - 1, place], recv_sem=sl_recv.at[d - 1, place],
             device_id={"bank": peer}, device_id_type=MESH,
         )
+
+    def slot_couple(d, g):
+        return slot_copy(d, g, g * 2 * kf, 2 * kf)
+
+    def slot_last(d, k):
+        return slot_copy(d, couples + k, (2 * couples + k) * kf, kf)
 
     def freq_copies(pairs_of, send, recv):
         copies = []
@@ -292,15 +301,38 @@
                     k * q + (sme * fshare if fsplit > 1 else 0) + r, i * kf, kf, weight,
                 )
 
-    def slots_off(rightward):
-        for dist in range(1, nb):
+    def send_slots(rightward, dists, low, high):
+        def send(dist, copy):
             there = me + dist < nb if rightward else me >= dist
 
             @pl.when(there)
             def _():
-                @pl.loop(0, fsteps)
-                def _(step):
-                    slot_copy(dist if rightward else nb - dist, step).start()
+                copy(dist if rightward else nb - dist).start()
+
+        @pl.loop(low, min(high, couples))
+        def _(g):
+            for dist in dists:
+                send(dist, lambda d: slot_couple(d, g))
+
+        if high > couples:
+            for k in range(2):
+                for dist in dists:
+                    send(dist, lambda d: slot_last(d, k))
+
+    def slots_off(rightward, end):
+        if end:
+            send_slots(rightward, [1], 0, couples + 1)
+            send_slots(rightward, range(2, nb), 0, couples + 1)
+        else:
+            send_slots(rightward, range(1, nb), 1, couples + 1)
+
+    @pl.when(me > 0)
+    def _():
+        send_slots(True, range(1, nb), 0, 1)
+
+    @pl.when(me < nb - 1)
+    def _():
+        send_slots(False, range(1, nb), 0, 1)
 
     def gathered_chunk(hop, c):
         @pl.when(me - 1 - hop >= 0)
@@ -323,21 +355,21 @@
 
             @pl.when(me == hop + 1)
             def _():
-                slots_off(True)
+                slots_off(True, False)
 
             @pl.when(nb - 1 - me == hop + 1)
             def _():
-                slots_off(False)
+                slots_off(False, False)
 
     @pl.when(me == 0)
     def _():
-        slots_off(True)
+        slots_off(True, True)
 
     @pl.when(me == nb - 1)
     def _():
-        slots_off(False)
-
-    events = [(hop, c) for hop in range(nb - 1) for c in range(chunks)]
+        slots_off(False, True)
+
+    events = [(hop, c) for hop in range(nb - 2) for c in range(chunks)]
     per = fsteps // csteps
     first = 2 * csteps // 8
 
@@ -410,16 +442,33 @@
         for k in range(nf):
             cacc[k] += out[k * crow : (k + 1) * crow]
 
+    def last_hop(c):
+        @pl.when(me == nb - 1)
+        def _():
+            ag_right(nb - 2, c, 0).wait_recv()
+
+        @pl.when(me == 0)
+        def _():
+            ag_left(nb - 2, c, nb - 1).wait_recv()
+
+    last_hop(0)
     coarse_lags(0, cbuf[0])
 
     @pl.loop(0, csteps // 2)
     def _(i):
+        @pl.when(i + 1 < chunks)
+        def _():
+            last_hop(i + 1)
+
         coarse_lags(2 * i + 1, cbuf[1])
         coarse_products(2 * i, cbuf[0])
         coarse_lags(jnp.minimum(2 * i + 2, csteps - 1), cbuf[0])
         coarse_products(2 * i + 1, cbuf[1])
 
-    coarse_copies = freq_copies(((cacc, crecv),), cx_send, cx_recv)
+    for d in range(1, nf):
+        peer = lax.rem(fme + d, nf)
+        csend[peer] = cacc[peer].astype(BF16)
+    coarse_copies = freq_copies(((csend, crecv),), cx_send, cx_recv)
     for copy in coarse_copies:
         copy.start()
 
@@ -489,23 +538,29 @@
         left = jnp.concatenate([ftemp_v[0, 0, :, window], ftemp_v[1, 0, :, window]], axis=0)
         facc[...] += nt_dot(left, buf[...])
 
-    def slots_here(step):
+    def slots_here(copy, at):
         for d in range(1, nb):
-            slot_copy(d, step).wait_recv()
-
-    slots_here(0)
+            copy(d, at).wait_recv()
+
+    slots_here(slot_couple, 0)
     fine_lags(0, fl0)
 
     @pl.loop(0, fsteps // 2 - 1)
     def _(i):
-        slots_here(2 * i + 1)
-        slots_here(2 * i + 2)
+        @pl.when(i + 1 < couples)
+        def _():
+            slots_here(slot_couple, i + 1)
+
+        @pl.when(i + 1 == couples)
+        def _():
+            slots_here(slot_last, 0)
+
         fine_lags(2 * i + 1, fl1)
         fine_products(2 * i, fl0)
         fine_lags(2 * i + 2, fl0)
         fine_products(2 * i + 1, fl1)
 
-    slots_here(fsteps - 1)
+    slots_here(slot_last, 1)
     fine_lags(fsteps - 1, fl1)
     fine_products(fsteps - 2, fl0)
     fine_products(fsteps - 1, fl1)
@@ -534,8 +589,8 @@
     for d in range(nf - 1):
         re = re + frecv[d, 0]
         im = im + frecv[d, 1]
-    top = peak(re * re + im * im, rows)[:, :128]
-    fsnr[...] = top / whole_norm(fnall)
+    ratio = jnp.transpose((re * re + im * im) / whole_norm(fnall))
+    fsnr[...] = jnp.max(ratio.reshape(LF, rows, q), axis=0)
     bcopies = back_copies()
     for copy in bcopies:
         copy.start()
@@ -545,7 +600,7 @@
         copy.wait_recv()
     acc = cacc[fme]
     for d in range(nf - 1):
-        acc = acc + crecv[d]
+        acc = acc + crecv[d].astype(F32)
     re, im = acc[:, :nc], acc[:, nc:]
     top = peak(re * re + im * im, segs)
     csnr[...] = jnp.transpose(top[:, :128] / whole_norm(cnall))[:segs]
@@ -563,25 +618,24 @@
             def _():
                 ag_left(hop, c).wait_send()
 
-    @pl.loop(0, fsteps)
-    def _(step):
+    @pl.loop(0, couples)
+    def _(g):
         for d in range(1, nb):
-            slot_copy(d, step).wait_send()
+            slot_couple(d, g).wait_send()
+
+    for k in range(2):
+        for d in range(1, nb):
+            slot_last(d, k).wait_send()
 
     for copy in bcopies:
         copy.wait()
-    at = lax.broadcasted_iota(I32, back.shape[1:], 1)
-    gathered = jnp.zeros(back.shape[1:], F32)
-    for b in range(nb):
-        turned = pltpu.roll(back[b], lax.rem((b - me + nb) * CAP + 128 - nb * CAP, 128), 1)
-        gathered = jnp.where((at >= b * CAP) & (at < (b + 1) * CAP), turned, gathered)
-    pair_at = lax.broadcasted_iota(I32, (pairs, 128), 0)
-    place = jnp.zeros((pairs, 128), I32)
+    pair_at = lax.broadcasted_iota(I32, (pairs, nb * rows), 0)
+    place = jnp.zeros(pair_at.shape, I32)
     for p in range(pairs):
-        place = jnp.where(pair_at == p, own[p] * CAP + own_rank[p], place)
-    giver = jnp.where(lax.broadcasted_iota(I32, (pairs, 128), 1) == place, 1.0, 0.0)
+        place = jnp.where(pair_at == p, own[p] * rows + me * CAP + own_rank[p], place)
+    giver = jnp.where(lax.broadcasted_iota(I32, place.shape, 1) == place, 1.0, 0.0)
     fout[...] = lax.dot_general(
-        giver, gathered, (((1,), (1,)), ((), ())),
+        giver, back[...].reshape(nb * rows, q), (((1,), (0,)), ((), ())),
         precision=lax.Precision.HIGHEST, preferred_element_type=F32,
     )
 
@@ -609,7 +663,7 @@
     segs = nb * seg_local
     kc = min(1024, cbins // 2)
     kf = min(2048, fbins // 2)
-    chunks = 4
+    chunks = cbins // kc // 2
     csteps = cbins // kc
     fsteps = fbins // kf
     crow = ctemps // nf
@@ -629,8 +683,8 @@
     csnr, fine_rows = pl.pallas_call(
         functools.partial(kernel, (nb, nf, ns, fsplit, kc, kf, chunks, period)),
         out_shape=(
-            jax.ShapeDtypeStruct((segs, crow), F32),
-            jax.ShapeDtypeStruct((seg_local * top_count, q), F32),
+            pltpu.VMEM((segs, crow), F32),
+            pltpu.VMEM((seg_local * top_count, q), F32),
         ),
         in_specs=[anywhere] * 10,
         out_specs=(vmem, vmem),
@@ -657,9 +711,10 @@
             pltpu.VMEM((nf, 2, q, nfl), F32),
             pltpu.VMEM((nf, q // fsplit, 128), F32),
             pltpu.VMEM((nf, fsplit, q // fsplit, 128), F32),
-            pltpu.VMEM((q, 128), F32),
-            pltpu.VMEM((nb, q, 128), F32),
-            pltpu.VMEM((nf - 1, crow, 2 * nc), F32),
+            pltpu.VMEM((rows, q), F32),
+            pltpu.VMEM((nb, rows, q), F32),
+            pltpu.VMEM((nf, crow, 2 * nc), BF16),
+            pltpu.VMEM((nf - 1, crow, 2 * nc), BF16),
             pltpu.VMEM((nf - 1, 2, q, nfl), F32),
             dma((8,)),
             dma((csteps,)),
@@ -668,8 +723,8 @@
             dma((nb - 1, chunks)),
             dma((nb - 1, chunks)),
             dma((nb - 1, chunks)),
-            dma((nb - 1, fsteps)),
-            dma((nb - 1, fsteps)),
+            dma((nb - 1, fsteps // 2 + 1)),
+            dma((nb - 1, fsteps // 2 + 1)),
             dma((nf - 1, 1)),
             dma((nf - 1, 1)),
             dma((nf * ns, 2)),

time: 54 us -> 47.7 us (0.88)
  Pallas kernels: 50.5 us -> 45.7 us
  local copies, waits for them, and re-layouts: 2.59 us -> 1.2 us
    pallas_call x1, Pallas kernels: 50.5 us -> 45.7 us  [body(): pl.pallas_call(functools.partial(kernel, (nb, nf, ns, fsplit, kc, kf, chu...]
    unnamed x2, local copies, waits for them, and re-layouts: 2.59 us -> 1.2 us
where the time goes in v3:
time: 47.7 us; the launch traced here: 47.6 us
  Pallas kernels  45.7 us (96%)
  local copies, waits for them, and re-layouts  1.2 us (3%)
  between operations  0.64 us (1%)
    pallas_call x1, Pallas kernels, body(): pl.pallas_call(functools.partial(kernel, (nb, nf, ns, fsplit, kc, kf, chu...  45.7 us
    unnamed x2, local copies, waits for them, and re-layouts  1.2 us

profile of v3, /device:TPU:0, one launch (start us, length us, event | category | flops | bytes accessed | tf_op | source)
XLA Modules:
  0.0 47.6 jit_solution(3368239545513249682)
XLA Ops:
  0.6 45.7 %shard_map.113 = (f32[16,256]{1,0:T(8,128)S(1)}, f32[8,32]{1,0:T(8,128)S(1)}) custom-call(s32[2,16]{1,0:T(2,128)} %bitcast.10, s32[2,16]{1,0:T(2,128)} %bitcast.11, bf16[4,2,8192]{2,1,0:T(2,128)(2,1)} %refs_2_.1, bf16[4,2,32768]{2,1,0:T(2,128)(2,1)} %refs_3_.1, bf16[2,512,8192]{2,1,0:T(8,128)(2,1)} %refs_4_.1, bf16[2,1,64,32768]{3,2,1,0:T(8,128)(2,1)} %refs_5_.1, ...), custom_call_target="tpu_custom_call" | custom-call | tf_op jit(solution)/shard_map/pallas_call | solution.py:683
  46.4 0.6 %copy.14 = f32[256,16]{0,1:T(8,128)} copy(f32[256,16]{0,1:T(8,128)S(1)} %bitcast.6) | data formatting | bytes 32768
  47.0 0.6 %copy.15 = f32[4,2,32]{2,1,0:T(2,128)} copy(f32[4,2,32]{2,1,0:T(2,128)S(1)} %bitcast.7) | data formatting | bytes 2048

commit v4 on v3

--- a/solution.py
+++ b/solution.py
@@ -63,7 +63,7 @@
         ag, outgoing, slots,
         cre0, cim0, cnre0, cre1, cim1, cnre1, fl0, fl1,
         cacc, cnorm, cnall, facc, fsum, fnorm, fnall, fsnr, back,
-        csend, crecv, frecv,
+        crecv, frecv,
         in_sem, ct_sem, ft_sem,
         agr_send, agr_recv, agl_send, agl_recv, sl_send, sl_recv,
         cx_send, cx_recv, nx_send, nx_recv, fx_send, fx_recv, bk_send, bk_recv,
@@ -371,7 +371,7 @@
 
     events = [(hop, c) for hop in range(nb - 2) for c in range(chunks)]
     per = fsteps // csteps
-    first = 2 * csteps // 8
+    first = 3 * csteps // 8
 
     @pl.loop(0, csteps)
     def _(i):
@@ -465,10 +465,7 @@
         coarse_lags(jnp.minimum(2 * i + 2, csteps - 1), cbuf[0])
         coarse_products(2 * i + 1, cbuf[1])
 
-    for d in range(1, nf):
-        peer = lax.rem(fme + d, nf)
-        csend[peer] = cacc[peer].astype(BF16)
-    coarse_copies = freq_copies(((csend, crecv),), cx_send, cx_recv)
+    coarse_copies = freq_copies(((cacc, crecv),), cx_send, cx_recv)
     for copy in coarse_copies:
         copy.start()
 
@@ -600,7 +597,7 @@
         copy.wait_recv()
     acc = cacc[fme]
     for d in range(nf - 1):
-        acc = acc + crecv[d].astype(F32)
+        acc = acc + crecv[d]
     re, im = acc[:, :nc], acc[:, nc:]
     top = peak(re * re + im * im, segs)
     csnr[...] = jnp.transpose(top[:, :128] / whole_norm(cnall))[:segs]
@@ -713,8 +710,7 @@
             pltpu.VMEM((nf, fsplit, q // fsplit, 128), F32),
             pltpu.VMEM((rows, q), F32),
             pltpu.VMEM((nb, rows, q), F32),
-            pltpu.VMEM((nf, crow, 2 * nc), BF16),
-            pltpu.VMEM((nf - 1, crow, 2 * nc), BF16),
+            pltpu.VMEM((nf - 1, crow, 2 * nc), F32),
             pltpu.VMEM((nf - 1, 2, q, nfl), F32),
             dma((8,)),
             dma((csteps,)),
@@ -751,6 +747,28 @@
         ctable,
         ftable,
     )
+    def settle(c_in, f_in, c_out, f_out, sem):
+        copies = [
+            pltpu.make_async_copy(c_in, c_out, sem.at[0]),
+            pltpu.make_async_copy(f_in, f_out, sem.at[1]),
+        ]
+        for copy in copies:
+            copy.start()
+        for copy in copies:
+            copy.wait()
+
+    csnr, fine_rows = pl.pallas_call(
+        settle,
+        out_shape=(
+            jax.ShapeDtypeStruct(csnr.shape, F32), jax.ShapeDtypeStruct(fine_rows.shape, F32)
+        ),
+        in_specs=[vmem, vmem],
+        out_specs=(anywhere, anywhere),
+        scratch_shapes=[dma((2,))],
+    )(
+        pltpu.with_memory_space_constraint(csnr, pltpu.VMEM),
+        pltpu.with_memory_space_constraint(fine_rows, pltpu.VMEM),
+    )
     return (csnr.T, fine_rows.reshape(seg_local, top_count, q))
 
 

time: 47.7 us -> 46.9 us (0.983)
  local copies, waits for them, and re-layouts: 1.2 us -> 0 us
    unnamed x2 -> x0, local copies, waits for them, and re-layouts: 1.2 us -> none
    pallas_call x0 -> x1, Pallas kernels: none -> 0.63 us  [body(): pl.pallas_call(settle, out_shape=(jax.ShapeDtypeStruct(csnr.shape, F32),...]
where the time goes in v4:
time: 46.9 us; the launch traced here: 46.8 us
  Pallas kernels  46.1 us (98%)
  between operations  0.64 us (1%)
    pallas_call x1, Pallas kernels, body(): pl.pallas_call(functools.partial(kernel, (nb, nf, ns, fsplit, kc, kf, chu...  45.5 us

profile of v4, /device:TPU:0, one launch (start us, length us, event | category | flops | bytes accessed | tf_op | source)
XLA Modules:
  0.0 46.8 jit_solution(1616300487889632873)
XLA Ops:
  0.6 45.5 %shard_map.113 = (f32[16,256]{1,0:T(8,128)S(1)}, f32[8,32]{1,0:T(8,128)S(1)}) custom-call(s32[2,16]{1,0:T(2,128)} %bitcast.8, s32[2,16]{1,0:T(2,128)} %bitcast.9, bf16[4,2,8192]{2,1,0:T(2,128)(2,1)} %refs_2_.1, bf16[4,2,32768]{2,1,0:T(2,128)(2,1)} %refs_3_.1, bf16[2,512,8192]{2,1,0:T(8,128)(2,1)} %refs_4_.1, bf16[2,1,64,32768]{3,2,1,0:T(8,128)(2,1)} %refs_5_.1, ...), custom_call_target="tpu_custom_call" | custom-call | tf_op jit(solution)/shard_map/pallas_call | solution.py:680
  46.2 0.6 %shard_map.114 = (f32[16,256]{1,0:T(8,128)}, f32[8,32]{1,0:T(8,128)}) custom-call(f32[16,256]{1,0:T(8,128)S(1)} %get-tuple-element.6.c_in, f32[8,32]{1,0:T(8,128)S(1)} %get-tuple-element.7.f_in), custom_call_target="tpu_custom_call" | custom-call | tf_op jit(solution)/shard_map/pallas_call | solution.py:760

commit v5 on v4

--- a/solution.py
+++ b/solution.py
@@ -322,9 +322,9 @@
     def slots_off(rightward, end):
         if end:
             send_slots(rightward, [1], 0, couples + 1)
-            send_slots(rightward, range(2, nb), 0, couples + 1)
+            send_slots(rightward, range(nb - 1, 1, -1), 0, couples + 1)
         else:
-            send_slots(rightward, range(1, nb), 1, couples + 1)
+            send_slots(rightward, range(nb - 1, 0, -1), 1, couples + 1)
 
     @pl.when(me > 0)
     def _():
@@ -626,15 +626,10 @@
 
     for copy in bcopies:
         copy.wait()
-    pair_at = lax.broadcasted_iota(I32, (pairs, nb * rows), 0)
-    place = jnp.zeros(pair_at.shape, I32)
     for p in range(pairs):
-        place = jnp.where(pair_at == p, own[p] * rows + me * CAP + own_rank[p], place)
-    giver = jnp.where(lax.broadcasted_iota(I32, place.shape, 1) == place, 1.0, 0.0)
-    fout[...] = lax.dot_general(
-        giver, back[...].reshape(nb * rows, q), (((1,), (0,)), ((), ())),
-        precision=lax.Precision.HIGHEST, preferred_element_type=F32,
-    )
+        bank = jnp.clip(own[p], 0, nb - 1)
+        row = me * CAP + jnp.minimum(own_rank[p], CAP - 1)
+        fout[p : p + 1, :] = back[bank, pl.ds(row, 1), :]
 
 
 def body(

time: 46.9 us -> 46.5 us (level)
  no operation moved by 1% of the time
where the time goes in v5:
time: 46.5 us; the launch traced here: 46.4 us
  Pallas kernels  45.7 us (98%)
  between operations  0.64 us (1%)
    pallas_call x1, Pallas kernels, body(): pl.pallas_call(functools.partial(kernel, (nb, nf, ns, fsplit, kc, kf, chu...  45.1 us

profile of v5, /device:TPU:0, one launch (start us, length us, event | category | flops | bytes accessed | tf_op | source)
XLA Modules:
  0.0 46.4 jit_solution(4771484247763628993)
XLA Ops:
  0.6 45.1 %shard_map.113 = (f32[16,256]{1,0:T(8,128)S(1)}, f32[8,32]{1,0:T(8,128)S(1)}) custom-call(s32[2,16]{1,0:T(2,128)} %bitcast.8, s32[2,16]{1,0:T(2,128)} %bitcast.9, bf16[4,2,8192]{2,1,0:T(2,128)(2,1)} %refs_2_.1, bf16[4,2,32768]{2,1,0:T(2,128)(2,1)} %refs_3_.1, bf16[2,512,8192]{2,1,0:T(8,128)(2,1)} %refs_4_.1, bf16[2,1,64,32768]{3,2,1,0:T(8,128)(2,1)} %refs_5_.1, ...), custom_call_target="tpu_custom_call" | custom-call | tf_op jit(solution)/shard_map/pallas_call | solution.py:675
  45.7 0.6 %shard_map.114 = (f32[16,256]{1,0:T(8,128)}, f32[8,32]{1,0:T(8,128)}) custom-call(f32[16,256]{1,0:T(8,128)S(1)} %get-tuple-element.6.c_in, f32[8,32]{1,0:T(8,128)S(1)} %get-tuple-element.7.f_in), custom_call_target="tpu_custom_call" | custom-call | tf_op jit(solution)/shard_map/pallas_call | solution.py:755
